TPU v7x, 32 devices: a whole 2x2x4 slice. The times are simulated.
32 devices in a mesh: group: 2 (over y), dev: 16 (over z, x, core).
Axes of the slice: x: 2, y: 2, z: 4, core: 2. Of those that a mesh axis runs over, the one named last changes fastest.
Arguments:
- bin_index: int32 [131072, 128], P(('group', 'dev')), may hold values from 0 to 63
- gradient: bfloat16 [131072], P(('group', 'dev')), may hold values from -6 to 6
- hessian: bfloat16 [131072], P(('group', 'dev')), may hold values from 0.049804688 to 0.25
- child_id: int32 [131072], P(('group', 'dev')), may hold values from 0 to 63
- smaller_side: int32 [32], replicated, may hold values from 0 to 1
Outputs:
- best_gain: float32 [32, 128], P('group', 'dev')
- child_best: float32 [32], P('group')
All inputs are finite; a program needn't handle non-finite values.
Results may differ from a plain program's by a relative error of at most 0.0003.
Values sent between devices are 32-bit elements; how exact they have to be, the bound alone decides.
A program may use at most 64 MiB of HBM per device.

v0:
```python
import math

import jax
import jax.numpy as jnp
from jax import lax
from jax.sharding import PartitionSpec as P

BINS = 64


reg_lambda = 1.0


def split_gains(hist_grad, hist_hess):
    left_grad = jnp.cumsum(hist_grad, axis=-1)[..., :-1]
    left_hess = jnp.cumsum(hist_hess, axis=-1)[..., :-1]
    total_grad = jnp.sum(hist_grad, axis=-1, keepdims=True)
    total_hess = jnp.sum(hist_hess, axis=-1, keepdims=True)
    right_grad = total_grad - left_grad
    value = left_grad * left_grad / (left_hess + reg_lambda)
    value = value + right_grad * right_grad / (total_hess - left_hess + reg_lambda)
    value = value - total_grad * total_grad / (total_hess + reg_lambda)
    return jnp.max(value, axis=-1)


def build_block(bin_index, weights, count):
    block_size = math.gcd(count, 8)
    leaves = weights.shape[1] // 2
    levels = jnp.arange(BINS, dtype=jnp.int32)

    def one_block(number):
        columns = lax.dynamic_slice_in_dim(bin_index, number * block_size, block_size, 1)
        onehot = (columns[:, :, None] == levels[None, None, :]).astype(jnp.bfloat16)
        onehot = onehot.reshape(columns.shape[0], block_size * BINS)
        product = lax.dot_general(
            onehot, weights, (((0,), (0,)), ((), ())), preferred_element_type=jnp.float32
        )
        product = product.reshape(block_size, BINS, 2, leaves).transpose(0, 3, 2, 1)
        return product.reshape(block_size, leaves, 2 * BINS)

    stacked = lax.map(one_block, jnp.arange(count // block_size, dtype=jnp.int32))
    return stacked.reshape(count, leaves, 2 * BINS)


def body(bin_index, gradient, hessian, child_id, smaller_side):
    leaves = smaller_side.shape[0]
    features = bin_index.shape[1]
    target = 2 * jnp.arange(leaves, dtype=jnp.int32)[None, :] + smaller_side[None, :]
    chosen = child_id[:, None] == target
    nothing = jnp.zeros((), jnp.bfloat16)
    weights = jnp.concatenate(
        [
            jnp.where(chosen, gradient[:, None], nothing),
            jnp.where(chosen, hessian[:, None], nothing),
        ],
        axis=1,
    )
    local_rows = features // lax.axis_size("dev")
    owned = lax.psum_scatter(
        build_block(bin_index, weights, lax.axis_size("dev") * local_rows),
        "dev",
        scatter_dimension=0,
        tiled=True,
    )
    owned = lax.psum_scatter(owned, "group", scatter_dimension=1, tiled=True)
    hist_grad = owned[:, :, :BINS].transpose(1, 0, 2)
    hist_hess = owned[:, :, BINS:].transpose(1, 0, 2)
    best_gain = split_gains(hist_grad, hist_hess)
    child_best = lax.pmax(jnp.max(best_gain, axis=1), "dev")
    return (best_gain, child_best)


def solution(mesh):
    in_specs = (
        P(("group", "dev"), None),
        P(("group", "dev")),
        P(("group", "dev")),
        P(("group", "dev")),
        P(),
    )
    out_specs = (P("group", "dev"), P("group"))
    return jax.shard_map(body, mesh=mesh, in_specs=in_specs, out_specs=out_specs, check_vma=False)
```

profile of v0, /device:TPU:0, one launch (start us, length us, event | category | flops | bytes accessed | tf_op | source)
XLA Modules:
  0.0 234.7 jit_solution(12362565521212994104)
XLA Ops:
  7.9 2.0 copy.13
  10.1 93.9 %while.11 = (s32[]{:T(128)}, f32[16,8,32,128]{3,2,1,0:T(8,128)}, s32[16]{0:T(128)S(1)}, s32[4096,128]{0,1:T(8,128)S(1)}, bf16[4096,64]{0,1:T(8,128)(2,1)S(1)}, /...) while((s32[]{:T(128)}, f32[16,8,32,128]{3,2,1,0:T(8,128)}, s32[16]{0:T(128)S(1)}, ...), condition=%wide.region_1.2_spmd.clone, body=%wide.region_0.1_spmd.clone.sunk | while | flops 270532608 | bytes 6038171 | solution.py:41
  12.8 2.1 convolution_bitcast_fusion.2
  18.6 2.1 convolution_bitcast_fusion.2
  24.5 2.1 convolution_bitcast_fusion.2
  30.4 2.1 convolution_bitcast_fusion.2
  36.3 2.1 convolution_bitcast_fusion.2
  42.1 2.1 convolution_bitcast_fusion.2
  48.0 2.1 convolution_bitcast_fusion.2
  53.8 2.1 convolution_bitcast_fusion.2
  59.7 2.1 convolution_bitcast_fusion.2
  65.6 2.1 convolution_bitcast_fusion.2
  71.5 2.1 convolution_bitcast_fusion.2
  77.3 2.1 convolution_bitcast_fusion.2
  83.2 2.1 convolution_bitcast_fusion.2
  89.0 2.1 convolution_bitcast_fusion.2
  94.9 2.1 convolution_bitcast_fusion.2
  100.8 2.1 convolution_bitcast_fusion.2
  104.0 4.2 %copy.14 = f32[128,32,128]{2,0,1:T(8,128)} copy(f32[128,32,128]{2,1,0:T(8,128)} %bitcast.43) | data formatting | bytes 4194304 | tf_op jit(solution)/shard_map/reshape | solution.py:42
  108.2 64.6 %reduce-scatter.3.cloned.1.call-done = f32[8,32,128]{2,0,1:T(8,128)} async-done(((f32[128,32,128]{2,0,1:T(8,128)}), f32[8,32,128]{2,0,1:T(8,128)}) %reduce-scatter.3.cloned.1.call-update) | async-done | bytes 131088 | tf_op jit(solution)/shard_map/reduce_scatter | solution.py:59
  172.8 11.5 %reduce-scatter.5.cloned.1.call-done = f32[8,16,128]{2,0,1:T(8,128)} async-done(((f32[8,32,128]{2,0,1:T(8,128)}), f32[8,16,128]{2,0,1:T(8,128)}) %reduce-scatter.5.cloned.1.call-update) | async-done | bytes 65552 | tf_op jit(solution)/shard_map/reduce_scatter | solution.py:65
  185.3 3.5 %reduce_window_sum.17 = f32[16,8,64]{2,1,0:T(8,128)S(1)} reduce-window(f32[16,8,64]{2,1,0:T(8,128)S(1)} %get-tuple-element.78, f32[]{:T(128)} %constant.7.clone.1), window={size=1x1x64 pad=0_0x0_0x63_0}, to_apply=%region_4.5 | reduce-window | flops 516096 | bytes 65540 | tf_op jit(solution)/shard_map/jit(cumsum)/reduce_window_sum | solution.py:15
  188.8 3.5 %reduce_window_sum.18 = f32[16,8,64]{2,1,0:T(8,128)S(1)} reduce-window(f32[16,8,64]{2,1,0:T(8,128)S(1)} %get-tuple-element.79, f32[]{:T(128)} %constant.7.clone.1), window={size=1x1x64 pad=0_0x0_0x63_0}, to_apply=%region_5.6 | reduce-window | flops 516096 | bytes 65540 | tf_op jit(solution)/shard_map/jit(cumsum)/reduce_window_sum | solution.py:16
  194.4 33.4 %pmax.7 = f32[16]{0:T(128)} all-reduce(f32[16]{0:T(128)S(1)} %get-tuple-element.64), channel_id=1, replica_groups=mesh['group'=2,'dev'=16] {'dev'}, use_global_device_ids=true, to_apply=%region_10.11 | all-reduce | flops 16 | bytes 128 | tf_op jit(solution)/shard_map/pmax | solution.py:69
  (148 shorter events, 52.8 us)
Async XLA Ops:
  7.2 165.6 %reduce-scatter.3.cloned.1.call-start = ((), (), s32[]{:S(2)}) async-start(), calls=%async_computation.2 | async-start | bytes 2228224 | tf_op jit(solution)/shard_map/reduce_scatter | solution.py:59
  7.9 2.0 copy-start
  7.9 2.0 copy-start.1
  7.9 2.0 copy-start.2
  108.2 76.2 %reduce-scatter.5.cloned.1.call-start = ((), (), s32[]{:S(2)}) async-start(), calls=%async_computation.3 | async-start | bytes 196608 | tf_op jit(solution)/shard_map/reduce_scatter | solution.py:65
Sparse Core Ops, SparseCore 0:
  108.3 64.4 reduce-scatter.2
  175.0 9.2 reduce-scatter.4
where the time goes:
time: 235 us
  waiting for transfers between devices  76.1 us (32%)
  local copies, waits for them, and re-layouts  35.5 us (15%)
  matrix products  34.1 us (15%)
  blocking collectives  33.4 us (14%)
  other arithmetic  30.3 us (13%)
  between operations  14.1 us (6%)
  loops' own time  11 us (5%)
    reduce_scatter x1, waiting for transfers between devices, body(): lax.psum_scatter(build_block(bin_index, weights, lax.axis_size('dev') * l...  64.6 us
    dot_general x16, matrix products, one_block(): lax.dot_general(onehot, weights, (((0,), (0,)), ((), ())), preferred_elem...  34.1 us
    pmax x1, blocking collectives, body(): child_best = lax.pmax(jnp.max(best_gain, axis=1), 'dev')  33.4 us
    eq x16, other arithmetic, one_block(): onehot = (columns[:, :, None] == levels[None, None, :]).astype(jnp.bfloat16)  21.1 us
    reduce_scatter x1, waiting for transfers between devices, body(): owned = lax.psum_scatter(owned, 'group', scatter_dimension=1, tiled=True)  11.5 us
    another operation x1, loops' own time, build_block(): lax.map(one_block, jnp.arange(count // block_size, dtype=jnp.int32))  11 us
    dynamic_update_slice x16, local copies, waits for them, and re-layouts, build_block(): lax.map(one_block, jnp.arange(count // block_size, dtype=jnp.int32))  10.5 us
    dynamic_slice x16, local copies, waits for them, and re-layouts, build_block(): lax.map(one_block, jnp.arange(count // block_size, dtype=jnp.int32))  9.32 us
  transfers between devices with their start and end apart: 2, of which 2 were waited for; matrix products, arithmetic and copies ran while one was open for 0% of the time, Pallas kernels for 0%

commit v1 on v0

v1 whole, which is shorter than its diff:
```python
import functools

import jax
import jax.numpy as jnp
from jax import lax
from jax.experimental import pallas as pl
from jax.experimental.pallas import tpu as pltpu
from jax.sharding import PartitionSpec as P

BINS = 64
LANES = 128
KCHUNK = 1024


reg_lambda = 1.0


def split_gains(hist_grad, hist_hess):
    left_grad = jnp.cumsum(hist_grad, axis=-1)[..., :-1]
    left_hess = jnp.cumsum(hist_hess, axis=-1)[..., :-1]
    total_grad = jnp.sum(hist_grad, axis=-1, keepdims=True)
    total_hess = jnp.sum(hist_hess, axis=-1, keepdims=True)
    right_grad = total_grad - left_grad
    value = left_grad * left_grad / (left_hess + reg_lambda)
    value = value + right_grad * right_grad / (total_hess - left_hess + reg_lambda)
    value = value - total_grad * total_grad / (total_hess + reg_lambda)
    return jnp.max(value, axis=-1)


def plain_body(bin_index, gradient, hessian, child_id, smaller_side):
    leaves = smaller_side.shape[0]
    features = bin_index.shape[1]
    target = 2 * jnp.arange(leaves, dtype=jnp.int32)[None, :] + smaller_side[None, :]
    chosen = child_id[:, None] == target
    nothing = jnp.zeros((), jnp.bfloat16)
    weights = jnp.concatenate(
        [
            jnp.where(chosen, gradient[:, None], nothing),
            jnp.where(chosen, hessian[:, None], nothing),
        ],
        axis=1,
    )
    levels = jnp.arange(BINS, dtype=jnp.int32)

    def one_feature(column):
        onehot = (column[:, None] == levels[None, :]).astype(jnp.bfloat16)
        product = lax.dot_general(
            weights, onehot, (((0,), (0,)), ((), ())), preferred_element_type=jnp.float32
        )
        return product.reshape(2, leaves, BINS).transpose(1, 0, 2).reshape(leaves, 2 * BINS)

    stacked = lax.map(one_feature, bin_index.T)
    owned = lax.psum_scatter(stacked, "dev", scatter_dimension=0, tiled=True)
    owned = lax.psum_scatter(owned, "group", scatter_dimension=1, tiled=True)
    hist_grad = owned[:, :, :BINS].transpose(1, 0, 2)
    hist_hess = owned[:, :, BINS:].transpose(1, 0, 2)
    best_gain = split_gains(hist_grad, hist_hess)
    child_best = lax.pmax(jnp.max(best_gain, axis=1), "dev")
    return (best_gain, child_best)


def kernel(
    groups, devs, leaves,
    bins_ref, grad_ref, hess_ref, child_ref, side_ref,
    gain_ref, best_ref,
    bins_t, weights, pair_out, pair_in, mine_out, mine_in, best_out, best_in,
    pair_send, pair_recv, mine_send, mine_recv, best_send, best_recv,
):
    rows, features = bins_ref.shape
    own_features = features // devs
    own_leaves = leaves // groups
    width = 2 * own_leaves
    slots = LANES // width
    quads = own_features // slots
    chips = devs // 2
    me_g = lax.axis_index("group")
    me_d = lax.axis_index("dev")
    me_c = lax.rem(me_d, 2)
    me_j = lax.div(me_d, 2)
    barrier = pltpu.get_barrier_semaphore()

    def at(g, d):
        return {"group": g, "dev": d}

    greeted = 0
    for step in range(1, devs):
        other = lax.rem(me_d + step, devs)
        pl.semaphore_signal(barrier, inc=1, device_id=at(me_g, other), device_id_type=pl.DeviceIdType.MESH)
        greeted += 1
    for turn in range(1, groups):
        for step in range(chips):
            other = lax.rem(me_j + step, chips) * 2 + me_c
            pl.semaphore_signal(
                barrier, inc=1, device_id=at(lax.rem(me_g + turn, groups), other),
                device_id_type=pl.DeviceIdType.MESH,
            )
            greeted += 1

    columns = groups * LANES
    column = lax.broadcasted_iota(jnp.int32, (columns, 1), 0)
    within = lax.rem(column, width)
    leaf = lax.div(column, LANES) * own_leaves + lax.rem(within, own_leaves)
    target = jnp.zeros_like(leaf)
    for number in range(leaves):
        target = jnp.where(leaf == number, 2 * number + side_ref[number], target)
    is_grad = within < own_leaves
    step_rows = min(rows, 512)

    def prepare(number, carry):
        here = pl.ds(pl.multiple_of(number * step_rows, step_rows), step_rows)
        child = child_ref[:, here]
        grad = grad_ref[:, here].astype(jnp.float32)
        hess = hess_ref[:, here].astype(jnp.float32)
        value = jnp.where(is_grad, grad, hess)
        value = jnp.where(child == target, value, 0.0)
        weights[here, :] = value.T.astype(jnp.bfloat16)
        bins_t[:, here] = bins_ref[here, :].astype(jnp.float32).T
        return carry

    lax.fori_loop(0, rows // step_rows, prepare, 0)
    pl.semaphore_wait(barrier, greeted)

    chunk = min(rows, KCHUNK)
    pack = 16
    level = lax.broadcasted_iota(jnp.int32, (pack, chunk), 0).astype(jnp.float32).astype(jnp.bfloat16)
    one = jnp.ones((), jnp.bfloat16)
    zero = jnp.zeros((), jnp.bfloat16)
    lane = lax.broadcasted_iota(jnp.int32, (BINS, LANES), 1)

    def block(d):
        base = pl.multiple_of(d * own_features, own_features)
        total = None
        for start in range(0, rows, chunk):
            parts = []
            values = bins_t[pl.ds(base, own_features), start:start + chunk]
            for f in range(own_features):
                row = jnp.broadcast_to(values[f:f + 1, :], (pack, chunk)).astype(jnp.bfloat16)
                for low in range(0, BINS, pack):
                    parts.append(jnp.where(row == level + jnp.bfloat16(low), one, zero))
            onehot = jnp.concatenate(parts, axis=0)
            product = jnp.dot(onehot, weights[start:start + chunk, :], preferred_element_type=jnp.float32)
            total = product if total is None else total + product
        result = []
        for g in range(groups):
            for q in range(quads):
                piece = None
                for s in range(slots):
                    f = q * slots + s
                    here = total[f * BINS:(f + 1) * BINS, g * LANES:(g + 1) * LANES]
                    piece = here if piece is None else jnp.where(lane >= s * width, here, piece)
                result.append(piece)
        return result

    def pair_copy(j):
        return pltpu.make_async_remote_copy(
            src_ref=pair_out.at[j], dst_ref=pair_in.at[j],
            send_sem=pair_send.at[j], recv_sem=pair_recv.at[j],
            device_id=at(me_g, me_j * 2 + 1 - me_c), device_id_type=pl.DeviceIdType.MESH,
        )

    def mine_copy(j, turn):
        to_g = lax.rem(me_g + turn, groups)
        to_j = lax.rem(me_j + 1 + j, chips)
        return pltpu.make_async_remote_copy(
            src_ref=mine_out.at[j, to_g], dst_ref=mine_in.at[turn, j],
            send_sem=mine_send.at[turn, j], recv_sem=mine_recv.at[turn, j],
            device_id=at(to_g, to_j * 2 + me_c), device_id_type=pl.DeviceIdType.MESH,
        )

    def one_chip(j, carry):
        to_j = lax.rem(me_j + 1 + j, chips)
        pieces = block(to_j * 2 + 1 - me_c)
        for g in range(groups):
            for q in range(quads):
                pair_out[j, g, q * BINS:(q + 1) * BINS, :] = pieces[g * quads + q]
        pair_copy(j).start()
        pieces = block(to_j * 2 + me_c)
        pair_copy(j).wait()
        for g in range(groups):
            for q in range(quads):
                part = slice(q * BINS, (q + 1) * BINS)
                mine_out[j, g, part, :] = pieces[g * quads + q] + pair_in[j, g, part, :]
        for turn in range(1, groups):
            mine_copy(j, turn).start()

        @pl.when(j < chips - 1)
        def _():
            mine_copy(j, 0).start()

        return carry

    lax.fori_loop(0, chips, one_chip, 0)

    hist = mine_out[chips - 1, me_g]
    for turn in range(groups):
        for j in range(chips):
            if turn == 0 and j == chips - 1:
                continue
            mine_copy(j, turn).wait()
            hist = hist + mine_in[turn, j]

    bests = []
    for q in range(quads):
        left = hist[q * BINS:(q + 1) * BINS, :]
        shift = 1
        while shift < BINS:
            left = left + jnp.concatenate(
                [jnp.zeros((shift, LANES), jnp.float32), left[:BINS - shift, :]], axis=0
            )
            shift *= 2
        both = pltpu.roll(left, LANES - own_leaves, 1)
        left_grad, left_hess = left, both
        total_grad, total_hess = left[BINS - 1:, :], both[BINS - 1:, :]
        right_grad = total_grad - left_grad
        usable = lax.rem(lane, width) < own_leaves
        left_hess = jnp.where(usable, left_hess, 0.0)
        total_hess = jnp.where(usable[:1, :], total_hess, 0.0)
        value = left_grad * left_grad / (left_hess + reg_lambda)
        value = value + right_grad * right_grad / (total_hess - left_hess + reg_lambda)
        value = value - total_grad * total_grad / (total_hess + reg_lambda)
        row = lax.broadcasted_iota(jnp.int32, (BINS, LANES), 0)
        value = jnp.where(row < BINS - 1, value, -jnp.inf)
        bests.append(jnp.max(value, axis=0, keepdims=True))
    best = bests[0]
    for q in range(quads):
        gain_ref[q:q + 1, :] = bests[q]
        best = jnp.maximum(best, bests[q])
    best = jnp.broadcast_to(best, (8, LANES))
    move = width
    folded = best
    for s in range(1, slots):
        folded = jnp.maximum(folded, pltpu.roll(best, s * move, 1))
    best_out[...] = folded

    def best_copy(step):
        return pltpu.make_async_remote_copy(
            src_ref=best_out, dst_ref=best_in.at[step],
            send_sem=best_send.at[step], recv_sem=best_recv.at[step],
            device_id=at(me_g, lax.rem(me_d + step, devs)), device_id_type=pl.DeviceIdType.MESH,
        )

    for step in range(1, devs):
        best_copy(step).start()
    for step in range(1, devs):
        best_copy(step).wait()
        folded = jnp.maximum(folded, best_in[step])
    best_ref[...] = folded


def kernel_body(groups, devs, bin_index, gradient, hessian, child_id, smaller_side):
    rows, features = bin_index.shape
    leaves = smaller_side.shape[0]
    own_features = features // devs
    own_leaves = leaves // groups
    width = 2 * own_leaves
    slots = LANES // width
    quads = own_features // slots
    chips = devs // 2
    vmem = pl.BlockSpec(memory_space=pltpu.VMEM)
    gain, best = pl.pallas_call(
        functools.partial(kernel, groups, devs, leaves),
        out_shape=(
            jax.ShapeDtypeStruct((quads, LANES), jnp.float32),
            jax.ShapeDtypeStruct((8, LANES), jnp.float32),
        ),
        in_specs=[vmem, vmem, vmem, vmem, pl.BlockSpec(memory_space=pltpu.SMEM)],
        out_specs=(vmem, vmem),
        scratch_shapes=[
            pltpu.VMEM((features, rows), jnp.float32),
            pltpu.VMEM((rows, groups * LANES), jnp.bfloat16),
            pltpu.VMEM((chips, groups, quads * BINS, LANES), jnp.float32),
            pltpu.VMEM((chips, groups, quads * BINS, LANES), jnp.float32),
            pltpu.VMEM((chips, groups, quads * BINS, LANES), jnp.float32),
            pltpu.VMEM((groups, chips, quads * BINS, LANES), jnp.float32),
            pltpu.VMEM((8, LANES), jnp.float32),
            pltpu.VMEM((devs, 8, LANES), jnp.float32),
            pltpu.SemaphoreType.DMA((chips,)),
            pltpu.SemaphoreType.DMA((chips,)),
            pltpu.SemaphoreType.DMA((groups, chips)),
            pltpu.SemaphoreType.DMA((groups, chips)),
            pltpu.SemaphoreType.DMA((devs,)),
            pltpu.SemaphoreType.DMA((devs,)),
        ],
        compiler_params=pltpu.CompilerParams(
            collective_id=0, has_side_effects=True, vmem_limit_bytes=48 * 1024 * 1024
        ),
    )(
        bin_index, gradient.reshape(1, rows), hessian.reshape(1, rows),
        child_id.reshape(1, rows), smaller_side,
    )
    best_gain = gain.reshape(quads, slots, width)[:, :, :own_leaves]
    best_gain = best_gain.transpose(2, 0, 1).reshape(own_leaves, own_features)
    return (best_gain, best[0, :own_leaves])


def fits(groups, devs, leaves, features, rows):
    if devs % 2 or features % devs or leaves % groups:
        return False
    width = 2 * (leaves // groups)
    if LANES % width:
        return False
    slots = LANES // width
    own = features // devs
    return own % slots == 0 and own % 8 == 0 and rows % KCHUNK == 0 and devs <= 16


def solution(mesh):
    in_specs = (
        P(("group", "dev"), None),
        P(("group", "dev")),
        P(("group", "dev")),
        P(("group", "dev")),
        P(),
    )
    out_specs = (P("group", "dev"), P("group"))
    groups, devs = mesh.shape["group"], mesh.shape["dev"]

    def body(bin_index, gradient, hessian, child_id, smaller_side):
        rows, features = bin_index.shape
        args = (bin_index, gradient, hessian, child_id, smaller_side)
        if fits(groups, devs, smaller_side.shape[0], features, rows):
            return kernel_body(groups, devs, *args)
        return plain_body(*args)

    return jax.shard_map(body, mesh=mesh, in_specs=in_specs, out_specs=out_specs, check_vma=False)
```

time: 235 us -> 58.8 us (0.25)
  waiting for transfers between devices: 76.1 us -> 0 us
  Pallas kernels: 0 us -> 52.2 us
  matrix products: 34.1 us -> 0 us
  blocking collectives: 33.4 us -> 0 us
  other arithmetic: 30.3 us -> 0 us
  local copies, waits for them, and re-layouts: 35.5 us -> 5.56 us
  between operations: 14.1 us -> 0.65 us
  loops' own time: 11 us -> 0 us
    reduce_scatter x2 -> x0, waiting for transfers between devices: 76.1 us -> none  [the longest x1 64.6 us: body(): lax.psum_scatter(build_block(bin_index, weights, lax.axis_size('dev') * l...]
    pallas_call x0 -> x1, Pallas kernels: none -> 52.2 us  [kernel_body(): pl.pallas_call(functools.partial(kernel, groups, devs, leaves), out_shape...]
    dot_general x16 -> x0, matrix products: 34.1 us -> none  [one_block(): lax.dot_general(onehot, weights, (((0,), (0,)), ((), ())), preferred_elem...]
    pmax x1 -> x0, blocking collectives: 33.4 us -> none  [body(): child_best = lax.pmax(jnp.max(best_gain, axis=1), 'dev')]
    eq x16 -> x0, other arithmetic: 21.1 us -> none  [one_block(): onehot = (columns[:, :, None] == levels[None, None, :]).astype(jnp.bfloat16)]
    another operation x1 -> x0, loops' own time: 11 us -> none  [build_block(): lax.map(one_block, jnp.arange(count // block_size, dtype=jnp.int32))]
    dynamic_update_slice x16 -> x0, local copies, waits for them, and re-layouts: 10.5 us -> none  [build_block(): lax.map(one_block, jnp.arange(count // block_size, dtype=jnp.int32))]
    dynamic_slice x32 -> x0, local copies, waits for them, and re-layouts: 9.57 us -> none  [the longest x16 9.32 us: build_block(): lax.map(one_block, jnp.arange(count // block_size, dtype=jnp.int32))]
  transfers between devices with their start and end apart: 2 -> 0, of which waited for: 2 -> 0; matrix products, arithmetic and copies ran while one was open for 0% -> 0% of each run, Pallas kernels for 0% -> 0%
where the time goes in v1:
time: 58.8 us; the launch traced here: 58.4 us
  Pallas kernels  52.2 us (89%)
  local copies, waits for them, and re-layouts  5.56 us (9%)
  between operations  0.65 us (1%)
    pallas_call x1, Pallas kernels, kernel_body(): pl.pallas_call(functools.partial(kernel, groups, devs, leaves), out_shape...  52.2 us
    unnamed x6, local copies, waits for them, and re-layouts  2.96 us

profile of v1, /device:TPU:0, one launch (start us, length us, event | category | flops | bytes accessed | tf_op | source)
XLA Modules:
  0.0 58.4 jit_solution(16093403593306434023)
XLA Ops:
  0.6 0.7 %reshape.19.grad_ref = bf16[1,4096]{1,0:T(2,128)(2,1)S(1)} reshape(bf16[4096]{0:T(1024)(128)(2,1)} %param.6) | data formatting | bytes 16384 | tf_op jit(solution)/shard_map/reshape | solution.py:288
  1.3 0.7 %reshape.20.hess_ref = bf16[1,4096]{1,0:T(2,128)(2,1)S(1)} reshape(bf16[4096]{0:T(1024)(128)(2,1)} %param.7) | data formatting | bytes 16384 | tf_op jit(solution)/shard_map/reshape | solution.py:288
  2.1 0.0 copy-start
  2.1 1.6 %copy-done = s32[4096,128]{1,0:T(8,128)S(1)} copy-done((s32[4096,128]{1,0:T(8,128)S(1)}, s32[4096,128]{1,0:T(8,128)}, u32[]{:S(2)}) %copy-start) | copy-done | bytes 2097176
  3.6 0.0 copy-start.1
  3.7 0.7 %copy-done.1 = s32[4096]{0:T(1024)S(1)} copy-done((s32[4096]{0:T(1024)S(1)}, s32[4096]{0:T(1024)}, u32[]{:S(2)}) %copy-start.1) | copy-done | bytes 16408
  4.4 0.0 copy-start.2
  4.4 0.7 %copy-done.2 = s32[32]{0:T(128)S(1)} copy-done((s32[32]{0:T(128)S(1)}, s32[32]{0:T(128)}, u32[]{:S(2)}) %copy-start.2) | copy-done | bytes 152
  5.0 52.2 %shard_map.68 = (f32[2,128]{1,0:T(2,128)S(1)}, f32[8,128]{1,0:T(8,128)S(1)}) custom-call(s32[4096,128]{1,0:T(8,128)S(1)} %copy-done, bf16[1,4096]{1,0:T(2,128)(2,1)S(1)} %reshape.19.grad_ref, bf16[1,4096]{1,0:T(2,128)(2,1)S(1)} %reshape.20.hess_ref, s32[1,4096]{1,0:T(1,128)S(1)} %bitcast.7, s32[32]{0:T(128)S(1)} %copy-done.2), custom_call_target="tpu_custom_call" | custom-call | tf_op jit(solution)/shard_map/pallas_call | solution.py:260
  57.2 0.5 slice_bitcast_fusion
  57.7 0.7 %reshape.22 = f32[2,4,32]{2,1,0:T(4,128)} reshape(f32[2,128]{1,0:T(2,128)S(1)} %get-tuple-element.4) | data formatting | bytes 2048 | tf_op jit(solution)/shard_map/reshape | solution.py:291
Async XLA Ops:
  2.1 1.6 %copy-start = (s32[4096,128]{1,0:T(8,128)S(1)}, s32[4096,128]{1,0:T(8,128)}, u32[]{:S(2)}) copy-start(s32[4096,128]{1,0:T(8,128)} %bins_ref.1) | copy-start | bytes 6291460
  3.6 0.7 %copy-start.1 = (s32[4096]{0:T(1024)S(1)}, s32[4096]{0:T(1024)}, u32[]{:S(2)}) copy-start(s32[4096]{0:T(1024)} %param.8) | copy-start | bytes 49156
  4.4 0.7 %copy-start.2 = (s32[32]{0:T(128)S(1)}, s32[32]{0:T(128)}, u32[]{:S(2)}) copy-start(s32[32]{0:T(128)} %side_ref.1) | copy-start | bytes 388

commit v2 on v1

--- a/solution.py
+++ b/solution.py
@@ -63,8 +63,9 @@
     groups, devs, leaves,
     bins_ref, grad_ref, hess_ref, child_ref, side_ref,
     gain_ref, best_ref,
-    bins_t, weights, pair_out, pair_in, mine_out, mine_in, best_out, best_in,
-    pair_send, pair_recv, mine_send, mine_recv, best_send, best_recv,
+    bins_t, weights, pair_out, pair_in, side_out, side_in, mine, far_in, near_in, best_out, best_in,
+    pair_send, pair_recv, side_send, side_recv, far_send, far_recv, near_send, near_recv,
+    best_send, best_recv,
 ):
     rows, features = bins_ref.shape
     own_features = features // devs
@@ -77,6 +78,9 @@
     me_d = lax.axis_index("dev")
     me_c = lax.rem(me_d, 2)
     me_j = lax.div(me_d, 2)
+    planes = chips // 2
+    me_x = lax.rem(me_j, 2)
+    me_z = lax.div(me_j, 2)
     barrier = pltpu.get_barrier_semaphore()
 
     def at(g, d):
@@ -158,46 +162,106 @@
             device_id=at(me_g, me_j * 2 + 1 - me_c), device_id_type=pl.DeviceIdType.MESH,
         )
 
-    def mine_copy(j, turn):
+    def side_copy(k):
+        return pltpu.make_async_remote_copy(
+            src_ref=side_out.at[k], dst_ref=side_in.at[k],
+            send_sem=side_send.at[k], recv_sem=side_recv.at[k],
+            device_id=at(me_g, (me_z * 2 + 1 - me_x) * 2 + me_c), device_id_type=pl.DeviceIdType.MESH,
+        )
+
+    def far_copy(k, turn):
         to_g = lax.rem(me_g + turn, groups)
-        to_j = lax.rem(me_j + 1 + j, chips)
-        return pltpu.make_async_remote_copy(
-            src_ref=mine_out.at[j, to_g], dst_ref=mine_in.at[turn, j],
-            send_sem=mine_send.at[turn, j], recv_sem=mine_recv.at[turn, j],
-            device_id=at(to_g, to_j * 2 + me_c), device_id_type=pl.DeviceIdType.MESH,
-        )
-
-    def one_chip(j, carry):
-        to_j = lax.rem(me_j + 1 + j, chips)
-        pieces = block(to_j * 2 + 1 - me_c)
+        return pltpu.make_async_remote_copy(
+            src_ref=mine.at[k, to_g], dst_ref=far_in.at[turn, k],
+            send_sem=far_send.at[turn, k], recv_sem=far_recv.at[turn, k],
+            device_id=at(to_g, (lax.rem(me_z + 1 + k, planes) * 2 + me_x) * 2 + me_c),
+            device_id_type=pl.DeviceIdType.MESH,
+        )
+
+    def near_copy(turn):
+        to_g = lax.rem(me_g + turn, groups)
+        return pltpu.make_async_remote_copy(
+            src_ref=side_out.at[planes - 1, to_g], dst_ref=near_in.at[turn],
+            send_sem=near_send.at[turn], recv_sem=near_recv.at[turn],
+            device_id=at(to_g, (me_z * 2 + 1 - me_x) * 2 + me_c), device_id_type=pl.DeviceIdType.MESH,
+        )
+
+    def owner(j):
+        to_z = lax.rem(me_z + 1 + lax.div(j, 2), planes)
+        to_x = lax.rem(me_x + 1 + lax.rem(j, 2), 2)
+        return (to_z * 2 + to_x) * 2
+
+    def send_pair(j):
+        pieces = block(owner(j) + 1 - me_c)
         for g in range(groups):
             for q in range(quads):
                 pair_out[j, g, q * BINS:(q + 1) * BINS, :] = pieces[g * quads + q]
         pair_copy(j).start()
-        pieces = block(to_j * 2 + me_c)
-        pair_copy(j).wait()
-        for g in range(groups):
-            for q in range(quads):
-                part = slice(q * BINS, (q + 1) * BINS)
-                mine_out[j, g, part, :] = pieces[g * quads + q] + pair_in[j, g, part, :]
-        for turn in range(1, groups):
-            mine_copy(j, turn).start()
+
+    send_pair(0)
+
+    def one_step(j, carry):
+        k = lax.div(j, 2)
+        odd = lax.rem(j, 2)
 
         @pl.when(j < chips - 1)
         def _():
-            mine_copy(j, 0).start()
+            send_pair(j + 1)
+
+        pieces = block(owner(j) + me_c)
+        pair_copy(j).wait()
+
+        def put(ref):
+            for g in range(groups):
+                for q in range(quads):
+                    part = slice(q * BINS, (q + 1) * BINS)
+                    ref[k, g, part, :] = pieces[g * quads + q] + pair_in[j, g, part, :]
+
+        @pl.when(odd == 0)
+        def _():
+            put(side_out)
+
+            @pl.when(k < planes - 1)
+            def _():
+                side_copy(k).start()
+
+            @pl.when(k == planes - 1)
+            def _():
+                for turn in range(groups):
+                    near_copy(turn).start()
+
+            @pl.when(k > 0)
+            def _():
+                side_copy(k - 1).wait()
+                for g in range(groups):
+                    mine[k - 1, g] = mine[k - 1, g] + side_in[k - 1, g]
+                for turn in range(groups):
+                    far_copy(k - 1, turn).start()
+
+        @pl.when(odd == 1)
+        def _():
+            put(mine)
+
+            @pl.when(k == planes - 1)
+            def _():
+                for turn in range(1, groups):
+                    far_copy(planes - 1, turn).start()
 
         return carry
 
-    lax.fori_loop(0, chips, one_chip, 0)
-
-    hist = mine_out[chips - 1, me_g]
+    lax.fori_loop(0, chips, one_step, 0)
+
+    hist = mine[planes - 1, me_g]
+    for k in range(planes - 1):
+        for turn in range(groups):
+            far_copy(k, turn).wait()
+            hist = hist + far_in[turn, k]
     for turn in range(groups):
-        for j in range(chips):
-            if turn == 0 and j == chips - 1:
-                continue
-            mine_copy(j, turn).wait()
-            hist = hist + mine_in[turn, j]
+        near_copy(turn).wait()
+        hist = hist + near_in[turn]
+    for turn in range(1, groups):
+        far_copy(planes - 1, turn).wait()
+        hist = hist + far_in[turn, planes - 1]
 
     bests = []
     for q in range(quads):
@@ -256,6 +320,7 @@
     slots = LANES // width
     quads = own_features // slots
     chips = devs // 2
+    planes = chips // 2
     vmem = pl.BlockSpec(memory_space=pltpu.VMEM)
     gain, best = pl.pallas_call(
         functools.partial(kernel, groups, devs, leaves),
@@ -270,14 +335,21 @@
             pltpu.VMEM((rows, groups * LANES), jnp.bfloat16),
             pltpu.VMEM((chips, groups, quads * BINS, LANES), jnp.float32),
             pltpu.VMEM((chips, groups, quads * BINS, LANES), jnp.float32),
-            pltpu.VMEM((chips, groups, quads * BINS, LANES), jnp.float32),
-            pltpu.VMEM((groups, chips, quads * BINS, LANES), jnp.float32),
+            pltpu.VMEM((planes, groups, quads * BINS, LANES), jnp.float32),
+            pltpu.VMEM((planes, groups, quads * BINS, LANES), jnp.float32),
+            pltpu.VMEM((planes, groups, quads * BINS, LANES), jnp.float32),
+            pltpu.VMEM((groups, planes, quads * BINS, LANES), jnp.float32),
+            pltpu.VMEM((groups, quads * BINS, LANES), jnp.float32),
             pltpu.VMEM((8, LANES), jnp.float32),
             pltpu.VMEM((devs, 8, LANES), jnp.float32),
             pltpu.SemaphoreType.DMA((chips,)),
             pltpu.SemaphoreType.DMA((chips,)),
-            pltpu.SemaphoreType.DMA((groups, chips)),
-            pltpu.SemaphoreType.DMA((groups, chips)),
+            pltpu.SemaphoreType.DMA((planes,)),
+            pltpu.SemaphoreType.DMA((planes,)),
+            pltpu.SemaphoreType.DMA((groups, planes)),
+            pltpu.SemaphoreType.DMA((groups, planes)),
+            pltpu.SemaphoreType.DMA((groups,)),
+            pltpu.SemaphoreType.DMA((groups,)),
             pltpu.SemaphoreType.DMA((devs,)),
             pltpu.SemaphoreType.DMA((devs,)),
         ],
@@ -294,7 +366,7 @@
 
 
 def fits(groups, devs, leaves, features, rows):
-    if devs % 2 or features % devs or leaves % groups:
+    if devs % 4 or devs < 8 or features % devs or leaves % groups:
         return False
     width = 2 * (leaves // groups)
     if LANES % width:

time: 58.8 us -> 44.4 us (0.76)
  Pallas kernels: 52.2 us -> 37.8 us
    pallas_call x1, Pallas kernels: 52.2 us -> 37.8 us  [kernel_body(): pl.pallas_call(functools.partial(kernel, groups, devs, leaves), out_shape...]
where the time goes in v2:
time: 44.4 us; the launch traced here: 44 us
  Pallas kernels  37.8 us (85%)
  local copies, waits for them, and re-layouts  5.56 us (13%)
  between operations  0.65 us (1%)
    pallas_call x1, Pallas kernels, kernel_body(): pl.pallas_call(functools.partial(kernel, groups, devs, leaves), out_shape...  37.8 us
    unnamed x6, local copies, waits for them, and re-layouts  2.96 us

profile of v2, /device:TPU:0, one launch (start us, length us, event | category | flops | bytes accessed | tf_op | source)
XLA Modules:
  0.0 44.0 jit_solution(8435494466156258518)
XLA Ops:
  0.6 0.7 %reshape.19.grad_ref = bf16[1,4096]{1,0:T(2,128)(2,1)S(1)} reshape(bf16[4096]{0:T(1024)(128)(2,1)} %param.6) | data formatting | bytes 16384 | tf_op jit(solution)/shard_map/reshape | solution.py:360
  1.3 0.7 %reshape.20.hess_ref = bf16[1,4096]{1,0:T(2,128)(2,1)S(1)} reshape(bf16[4096]{0:T(1024)(128)(2,1)} %param.7) | data formatting | bytes 16384 | tf_op jit(solution)/shard_map/reshape | solution.py:360
  2.1 0.0 copy-start
  2.1 1.6 %copy-done = s32[4096,128]{1,0:T(8,128)S(1)} copy-done((s32[4096,128]{1,0:T(8,128)S(1)}, s32[4096,128]{1,0:T(8,128)}, u32[]{:S(2)}) %copy-start) | copy-done | bytes 2097176
  3.6 0.0 copy-start.1
  3.7 0.7 %copy-done.1 = s32[4096]{0:T(1024)S(1)} copy-done((s32[4096]{0:T(1024)S(1)}, s32[4096]{0:T(1024)}, u32[]{:S(2)}) %copy-start.1) | copy-done | bytes 16408
  4.4 0.0 copy-start.2
  4.4 0.7 %copy-done.2 = s32[32]{0:T(128)S(1)} copy-done((s32[32]{0:T(128)S(1)}, s32[32]{0:T(128)}, u32[]{:S(2)}) %copy-start.2) | copy-done | bytes 152
  5.0 37.8 %shard_map.68 = (f32[2,128]{1,0:T(2,128)S(1)}, f32[8,128]{1,0:T(8,128)S(1)}) custom-call(s32[4096,128]{1,0:T(8,128)S(1)} %copy-done, bf16[1,4096]{1,0:T(2,128)(2,1)S(1)} %reshape.19.grad_ref, bf16[1,4096]{1,0:T(2,128)(2,1)S(1)} %reshape.20.hess_ref, s32[1,4096]{1,0:T(1,128)S(1)} %bitcast.7, s32[32]{0:T(128)S(1)} %copy-done.2), custom_call_target="tpu_custom_call" | custom-call | tf_op jit(solution)/shard_map/pallas_call | solution.py:325
  42.9 0.5 %slice_bitcast_fusion = f32[16]{0:T(128)} fusion(f32[8,128]{1,0:T(8,128)S(1)} %get-tuple-element.5), kind=kLoop, calls=%fused_computation | loop fusion | bytes 128 | tf_op jit(solution)/shard_map/squeeze | solution.py:365
  43.4 0.7 %reshape.22 = f32[2,4,32]{2,1,0:T(4,128)} reshape(f32[2,128]{1,0:T(2,128)S(1)} %get-tuple-element.4) | data formatting | bytes 2048 | tf_op jit(solution)/shard_map/reshape | solution.py:363
Async XLA Ops:
  2.1 1.6 %copy-start = (s32[4096,128]{1,0:T(8,128)S(1)}, s32[4096,128]{1,0:T(8,128)}, u32[]{:S(2)}) copy-start(s32[4096,128]{1,0:T(8,128)} %bins_ref.1) | copy-start | bytes 6291460
  3.6 0.7 %copy-start.1 = (s32[4096]{0:T(1024)S(1)}, s32[4096]{0:T(1024)}, u32[]{:S(2)}) copy-start(s32[4096]{0:T(1024)} %param.8) | copy-start | bytes 49156
  4.4 0.7 %copy-start.2 = (s32[32]{0:T(128)S(1)}, s32[32]{0:T(128)}, u32[]{:S(2)}) copy-start(s32[32]{0:T(128)} %side_ref.1) | copy-start | bytes 388

commit v3 on v2

--- a/solution.py
+++ b/solution.py
@@ -10,6 +10,7 @@
 BINS = 64
 LANES = 128
 KCHUNK = 1024
+STEP_ROWS = 512
 
 
 reg_lambda = 1.0
@@ -63,6 +64,7 @@
     groups, devs, leaves,
     bins_ref, grad_ref, hess_ref, child_ref, side_ref,
     gain_ref, best_ref,
+    bins_v, grad_v, hess_v, child_v, values, bins_sem, small_sem,
     bins_t, weights, pair_out, pair_in, side_out, side_in, mine, far_in, near_in, best_out, best_in,
     pair_send, pair_recv, side_send, side_recv, far_send, far_recv, near_send, near_recv,
     best_send, best_recv,
@@ -82,6 +84,20 @@
     me_x = lax.rem(me_j, 2)
     me_z = lax.div(me_j, 2)
     barrier = pltpu.get_barrier_semaphore()
+    step_rows = STEP_ROWS
+
+    def bins_copy(number):
+        here = pl.ds(pl.multiple_of(number * step_rows, step_rows), step_rows)
+        return pltpu.make_async_copy(bins_ref.at[here, :], bins_v.at[here, :], bins_sem.at[number])
+
+    small = [
+        pltpu.make_async_copy(source, place, small_sem.at[number])
+        for number, (source, place) in enumerate(
+            [(grad_ref, grad_v), (hess_ref, hess_v), (child_ref, child_v)]
+        )
+    ]
+    for copy in small:
+        copy.start()
 
     def at(g, d):
         return {"group": g, "dev": d}
@@ -108,21 +124,26 @@
     for number in range(leaves):
         target = jnp.where(leaf == number, 2 * number + side_ref[number], target)
     is_grad = within < own_leaves
-    step_rows = min(rows, 512)
+
+    lax.fori_loop(0, rows // step_rows, lambda number, carry: (bins_copy(number).start(), carry)[1], 0)
+    for copy in small:
+        copy.wait()
+    values[0] = grad_v[...].astype(jnp.float32)
+    values[1] = hess_v[...].astype(jnp.float32)
 
     def prepare(number, carry):
+        bins_copy(number).wait()
         here = pl.ds(pl.multiple_of(number * step_rows, step_rows), step_rows)
-        child = child_ref[:, here]
-        grad = grad_ref[:, here].astype(jnp.float32)
-        hess = hess_ref[:, here].astype(jnp.float32)
-        value = jnp.where(is_grad, grad, hess)
-        value = jnp.where(child == target, value, 0.0)
-        weights[here, :] = value.T.astype(jnp.bfloat16)
-        bins_t[:, here] = bins_ref[here, :].astype(jnp.float32).T
+        bins_t[:, here] = bins_v[here, :].astype(jnp.float32).T
+        for piece in range(step_rows // LANES):
+            row = number * (step_rows // LANES) + piece
+            value = jnp.where(is_grad, values[0, pl.ds(row, 1), :], values[1, pl.ds(row, 1), :])
+            value = jnp.where(child_v[pl.ds(row, 1), :] == target, value, 0.0)
+            there = pl.ds(pl.multiple_of(row * LANES, LANES), LANES)
+            weights[there, :] = value.T.astype(jnp.bfloat16)
         return carry
 
     lax.fori_loop(0, rows // step_rows, prepare, 0)
-    pl.semaphore_wait(barrier, greeted)
 
     chunk = min(rows, KCHUNK)
     pack = 16
@@ -136,9 +157,9 @@
         total = None
         for start in range(0, rows, chunk):
             parts = []
-            values = bins_t[pl.ds(base, own_features), start:start + chunk]
+            levels = bins_t[pl.ds(base, own_features), start:start + chunk]
             for f in range(own_features):
-                row = jnp.broadcast_to(values[f:f + 1, :], (pack, chunk)).astype(jnp.bfloat16)
+                row = jnp.broadcast_to(levels[f:f + 1, :], (pack, chunk)).astype(jnp.bfloat16)
                 for low in range(0, BINS, pack):
                     parts.append(jnp.where(row == level + jnp.bfloat16(low), one, zero))
             onehot = jnp.concatenate(parts, axis=0)
@@ -191,14 +212,16 @@
         to_x = lax.rem(me_x + 1 + lax.rem(j, 2), 2)
         return (to_z * 2 + to_x) * 2
 
-    def send_pair(j):
+    def send_pair(j, first=False):
         pieces = block(owner(j) + 1 - me_c)
+        if first:
+            pl.semaphore_wait(barrier, greeted)
         for g in range(groups):
             for q in range(quads):
                 pair_out[j, g, q * BINS:(q + 1) * BINS, :] = pieces[g * quads + q]
         pair_copy(j).start()
 
-    send_pair(0)
+    send_pair(0, True)
 
     def one_step(j, carry):
         k = lax.div(j, 2)
@@ -322,15 +345,23 @@
     chips = devs // 2
     planes = chips // 2
     vmem = pl.BlockSpec(memory_space=pltpu.VMEM)
+    hbm = pl.BlockSpec(memory_space=pltpu.HBM)
     gain, best = pl.pallas_call(
         functools.partial(kernel, groups, devs, leaves),
         out_shape=(
             jax.ShapeDtypeStruct((quads, LANES), jnp.float32),
             jax.ShapeDtypeStruct((8, LANES), jnp.float32),
         ),
-        in_specs=[vmem, vmem, vmem, vmem, pl.BlockSpec(memory_space=pltpu.SMEM)],
+        in_specs=[hbm, hbm, hbm, hbm, pl.BlockSpec(memory_space=pltpu.SMEM)],
         out_specs=(vmem, vmem),
         scratch_shapes=[
+            pltpu.VMEM((rows, features), jnp.int32),
+            pltpu.VMEM((rows // LANES, LANES), jnp.bfloat16),
+            pltpu.VMEM((rows // LANES, LANES), jnp.bfloat16),
+            pltpu.VMEM((rows // LANES, LANES), jnp.int32),
+            pltpu.VMEM((2, rows // LANES, LANES), jnp.float32),
+            pltpu.SemaphoreType.DMA((rows // STEP_ROWS,)),
+            pltpu.SemaphoreType.DMA((3,)),
             pltpu.VMEM((features, rows), jnp.float32),
             pltpu.VMEM((rows, groups * LANES), jnp.bfloat16),
             pltpu.VMEM((chips, groups, quads * BINS, LANES), jnp.float32),
@@ -354,11 +385,11 @@
             pltpu.SemaphoreType.DMA((devs,)),
         ],
         compiler_params=pltpu.CompilerParams(
-            collective_id=0, has_side_effects=True, vmem_limit_bytes=48 * 1024 * 1024
+            collective_id=0, has_side_effects=True, vmem_limit_bytes=63 * 1024 * 1024
         ),
     )(
-        bin_index, gradient.reshape(1, rows), hessian.reshape(1, rows),
-        child_id.reshape(1, rows), smaller_side,
+        bin_index, gradient.reshape(rows // LANES, LANES), hessian.reshape(rows // LANES, LANES),
+        child_id.reshape(rows // LANES, LANES), smaller_side,
     )
     best_gain = gain.reshape(quads, slots, width)[:, :, :own_leaves]
     best_gain = best_gain.transpose(2, 0, 1).reshape(own_leaves, own_features)

time: 44.4 us -> 43 us (0.968)
  local copies, waits for them, and re-layouts: 5.56 us -> 2.51 us
  Pallas kernels: 37.8 us -> 39.5 us
    unnamed x6 -> x0, local copies, waits for them, and re-layouts: 2.96 us -> none
    pallas_call x1, Pallas kernels: 37.8 us -> 39.5 us  [kernel_body(): pl.pallas_call(functools.partial(kernel, groups, devs, leaves), out_shape...]
    reshape x2 -> x0, local copies, waits for them, and re-layouts: 1.42 us -> none  [the longest x1 0.71 us: kernel_body(): hessian.reshape(1, rows)]
    squeeze x1, local copies, waits for them, and re-layouts: 0.51 us -> 1.18 us  [kernel_body(): return (best_gain, best[0, :own_leaves])]
    reshape x1, local copies, waits for them, and re-layouts: 0.67 us -> 1.33 us  [kernel_body(): best_gain = gain.reshape(quads, slots, width)[:, :, :own_leaves]]
where the time goes in v3:
time: 43 us; the launch traced here: 42.7 us
  Pallas kernels  39.5 us (92%)
  local copies, waits for them, and re-layouts  2.51 us (6%)
  between operations  0.64 us (1%)
    pallas_call x1, Pallas kernels, kernel_body(): pl.pallas_call(functools.partial(kernel, groups, devs, leaves), out_shape...  39.5 us
    reshape x1, local copies, waits for them, and re-layouts, kernel_body(): best_gain = gain.reshape(quads, slots, width)[:, :, :own_leaves]  1.33 us
    squeeze x1, local copies, waits for them, and re-layouts, kernel_body(): return (best_gain, best[0, :own_leaves])  1.18 us

profile of v3, /device:TPU:0, one launch (start us, length us, event | category | flops | bytes accessed | tf_op | source)
XLA Modules:
  0.0 42.7 jit_solution(1280069303370376417)
XLA Ops:
  0.6 39.5 %shard_map.68 = (f32[2,128]{1,0:T(2,128)}, f32[8,128]{1,0:T(8,128)}) custom-call(s32[4096,128]{1,0:T(8,128)} %bins_ref.1, bf16[32,128]{1,0:T(8,128)(2,1)} %bitcast.10, bf16[32,128]{1,0:T(8,128)(2,1)} %bitcast.11, s32[32,128]{1,0:T(8,128)} %bitcast.9, s32[32]{0:T(128)} %side_ref.1), custom_call_target="tpu_custom_call" | custom-call | tf_op jit(solution)/shard_map/pallas_call | solution.py:349
  40.2 1.2 %slice_bitcast_fusion = f32[16]{0:T(128)} fusion(f32[8,128]{1,0:T(8,128)} %get-tuple-element.5), kind=kLoop, calls=%fused_computation | loop fusion | bytes 128 | tf_op jit(solution)/shard_map/squeeze | solution.py:396
  41.4 1.3 %reshape.22 = f32[2,4,32]{2,1,0:T(4,128)} reshape(f32[2,128]{1,0:T(2,128)} %get-tuple-element.4) | data formatting | bytes 2048 | tf_op jit(solution)/shard_map/reshape | solution.py:394
